TPU v7x, 32 devices: a whole 2x2x4 slice. The times are simulated.
32 devices in a mesh: cohort: 2 (over x), tile: 16 (over z, y, core).
Axes of the slice: x: 2, y: 2, z: 4, core: 2. Of those that a mesh axis runs over, the one named last changes fastest.
Arguments:
- dosage: bfloat16 [512, 8192], P(('cohort', 'tile')), parts along dimension 0, may hold values from 0 to 2
- covars: float32 [512, 16], P(('cohort', 'tile')), parts along dimension 0, may hold values from -12 to 12, as said below
- phenotypes: float32 [512, 1792], P(('cohort', 'tile')), parts along dimension 0, may hold values from -100 to 100
Outputs:
- mean_chi: float32 [3584], P(('cohort', 'tile')), parts along dimension 0
- hit_rate: float32 [3584], P(('cohort', 'tile')), parts along dimension 0
There are 2 independent parts, one for each index of `cohort`. A program takes and returns all parts, laid end to end along the dimension named above; each array names one. Nothing has to cross between parts.
Inputs may be any that keep to these rules, and one draw needn't show every extreme that they name: `covars`: each covariate column has its own mean and spread.
All inputs are finite; a program needn't handle non-finite values.
Results may differ from a plain program's by a relative error of at most 0.003.
Values may be sent and summed in bfloat16 or wider, within the bound.
A program may use at most 64 MiB of HBM per device.

v0:
```python
import jax
import jax.numpy as jnp
from jax import lax
from jax.sharding import PartitionSpec as P


def local(dosage, covars, phenotypes):
    highest = lax.Precision.HIGHEST
    devices = lax.axis_size("tile")
    local_rows = dosage.shape[0]
    variants = dosage.shape[1]
    samples = local_rows * devices
    genes_all = phenotypes.shape[1]
    gene_own = genes_all // devices
    scale_root = jnp.sqrt(jnp.float32(samples))
    covars_all = lax.all_gather(covars, "tile", axis=0, tiled=True)
    dose_all = lax.all_gather(dosage, "tile", axis=0, tiled=True)
    pheno_own = lax.all_to_all(phenotypes, "tile", split_axis=1, concat_axis=0, tiled=True)
    gram = jnp.dot(covars_all.T, covars_all, precision=highest, preferred_element_type=jnp.float32)
    factor = jnp.linalg.cholesky(gram)
    cov_pheno = jnp.dot(
        covars_all.T, pheno_own, precision=highest, preferred_element_type=jnp.float32
    )
    beta_pheno = jax.scipy.linalg.cho_solve((factor, True), cov_pheno)
    pheno_resid = pheno_own - jnp.dot(
        covars_all, beta_pheno, precision=highest, preferred_element_type=jnp.float32
    )
    pheno_sumsq = jnp.sum(pheno_resid * pheno_resid, axis=0)
    pheno_bf = pheno_resid.astype(jnp.bfloat16)
    pheno_var = pheno_sumsq / samples + 0.1
    width = 1024
    blocks = variants // width

    def one_block(index, totals):
        start = index * width
        dose_block = lax.dynamic_slice_in_dim(dose_all, start, width, 1).astype(jnp.float32)
        cov_dose = jnp.dot(
            covars_all.T, dose_block, precision=highest, preferred_element_type=jnp.float32
        )
        beta_dose = jax.scipy.linalg.cho_solve((factor, True), cov_dose)
        dose_resid = dose_block - jnp.dot(
            covars_all, beta_dose, precision=highest, preferred_element_type=jnp.float32
        )
        dose_var = jnp.sum(dose_resid * dose_resid, axis=0) / samples + 0.1
        cross = lax.dot_general(
            pheno_bf,
            dose_resid.astype(jnp.bfloat16),
            (((0,), (0,)), ((), ())),
            preferred_element_type=jnp.float32,
        )
        zscore = cross / (scale_root * jnp.sqrt(pheno_var[:, None] * dose_var[None, :]))
        chi_square = zscore * zscore
        return (
            totals[0] + jnp.sum(chi_square, axis=1),
            totals[1] + jnp.sum(jax.nn.sigmoid(2.0 * (chi_square - 4.0)), axis=1),
        )

    zeros = jnp.zeros((gene_own,), jnp.float32)
    chi_total, hit_total = lax.fori_loop(0, blocks, one_block, (zeros, zeros))
    return (chi_total / variants, 20.0 / variants * hit_total)


def solution(mesh):
    return jax.shard_map(
        local,
        mesh=mesh,
        in_specs=(
            P(("cohort", "tile"), None),
            P(("cohort", "tile"), None),
            P(("cohort", "tile"), None),
        ),
        out_specs=(P(("cohort", "tile")), P(("cohort", "tile"))),
        check_vma=False,
    )
```

profile of v0, /device:TPU:0, one launch (start us, length us, event | category | flops | bytes accessed | tf_op | source)
XLA Modules:
  0.0 117.5 jit_solution(11533161251048784845)
XLA Ops:
  7.9 1.0 all_to_all.14
  8.9 0.7 copy.15
  9.6 7.4 %all-to-all-start = ((f32[16,16,112]{2,0,1:T(8,128)}), f32[16,16,112]{2,0,1:T(8,128)S(1)}, u32[]{:S(2)}, u32[]{:S(2)}) async-start(f32[16,16,112]{2,0,1:T(8,128)} %copy.15), calls=%async_computation | async-start | bytes 262144 | tf_op jit(solution)/shard_map/all_to_all | solution.py:18
  17.0 22.7 %all_gather.7 = f32[256,16]{1,0:T(8,128)S(1)} all-gather(f32[16,16]{1,0:T(8,128)} %param.6), channel_id=1, replica_groups=mesh['cohort'=2,'tile'=16] {'tile'}, dimensions={0}, use_global_device_ids=true | all-gather | bytes 17408 | tf_op jit(solution)/shard_map/all_gather | solution.py:16
  40.2 1.5 %cholesky.18 = f32[16,16]{1,0:T(8,128)S(1)} custom-call(f32[16,16]{1,0:T(8,128)S(1)} %fusion.19), custom_call_target="Cholesky" | custom-call | tf_op jit(solution)/shard_map/jit(cholesky)/cholesky | solution.py:20
  43.0 1.2 %custom-call.24 = f32[1,16,16]{1,2,0:T(8,128)S(1)} custom-call(f32[1,16,16]{2,1,0:T(8,128)S(1)} %get-tuple-element.272), custom_call_target="InvertDiagBlocksLowerTriangular" | custom-call | tf_op jit(solution)/shard_map/jit(_cho_solve)/triangular_solve | solution.py:24
  45.6 18.0 %all-gather.2.cloned.1.call-done = bf16[256,8192]{1,0:T(8,128)(2,1)} async-done(((bf16[16,8192]{1,0:T(8,128)(2,1)}), bf16[256,8192]{1,0:T(8,128)(2,1)}) %all-gather.2.cloned.1.call-update) | async-done | bytes 4194320 | tf_op jit(solution)/shard_map/all_gather | solution.py:17
  63.6 46.5 %while.18 = (s32[]{:T(128)}, f32[112]{0:T(128)S(1)}, f32[112]{0:T(128)S(1)}, bf16[256,8192]{1,0:T(8,128)(2,1)}, f32[16,16]{1,0:T(8,128)S(1)}, /*index=5*/f32[256...) while((s32[]{:T(128)}, f32[112]{0:T(128)S(1)}, ...), condition=%wide.region_7.8_spmd.clone, body=%wide.region_3.7_spmd.clone.sunk | while | flops 168249056 | bytes 2605173 | solution.py:59
  63.6 1.4 %fusion.62 = f32[1024,16]{0,1:T(8,128)S(1)} fusion(f32[256,16]{0,1:T(8,128)S(1)} %get-tuple-element.375, bf16[256,8192]{1,0:T(8,128)(2,1)} %get-tuple-element.373, s32[]{:T(128)S(6)} %select_n.19), kind=kOutput, calls=%fused_computation.7.clone.1 | convolution fusion | flops 50331648 | bytes 606212 | tf_op jit(solution)/shard_map/while/body/eval_jaxpr/dot_general | solution.py:37
  65.0 1.2 %custom-call.29 = f32[1,16,16]{1,2,0:T(8,128)S(1)} custom-call(f32[1,16,16]{2,1,0:T(8,128)S(1)} %bitcast_select_fusion.2), custom_call_target="InvertDiagBlocksLowerTriangular" | custom-call | tf_op jit(solution)/shard_map/while/body/eval_jaxpr/jit(_cho_solve)/triangular_solve | solution.py:40
  66.7 2.1 %multiply_reduce_fusion.3 = (f32[1024]{0:T(1024)S(1)}, bf16[256,1024]{1,0:T(8,128)(2,1)S(1)}) fusion(f32[16,1024]{1,0:T(8,128)S(1)} %fusion.64, f32[256,16]{0,1:T(8,128)S(1)} %get-tuple-element.375, bf16[256,8192]{1,0:T(8,128)(2,1)} %get-tuple-element.373, s32[]{:T(128)S(6)} %select_n.19), kind=kOutput, calls=%fused_computation.5.clone.1 | convolution fusion | flops 51641344 | bytes 1134596 | tf_op jit(solution)/shard_map/while/body/eval_jaxpr/dot_general | solution.py:41
  69.4 1.4 %fusion.62 = f32[1024,16]{0,1:T(8,128)S(1)} fusion(f32[256,16]{0,1:T(8,128)S(1)} %get-tuple-element.375, bf16[256,8192]{1,0:T(8,128)(2,1)} %get-tuple-element.373, s32[]{:T(128)S(6)} %select_n.19), kind=kOutput, calls=%fused_computation.7.clone.1 | convolution fusion | flops 50331648 | bytes 606212 | tf_op jit(solution)/shard_map/while/body/eval_jaxpr/dot_general | solution.py:37
  70.8 1.2 %custom-call.29 = f32[1,16,16]{1,2,0:T(8,128)S(1)} custom-call(f32[1,16,16]{2,1,0:T(8,128)S(1)} %bitcast_select_fusion.2), custom_call_target="InvertDiagBlocksLowerTriangular" | custom-call | tf_op jit(solution)/shard_map/while/body/eval_jaxpr/jit(_cho_solve)/triangular_solve | solution.py:40
  72.5 2.1 %multiply_reduce_fusion.3 = (f32[1024]{0:T(1024)S(1)}, bf16[256,1024]{1,0:T(8,128)(2,1)S(1)}) fusion(f32[16,1024]{1,0:T(8,128)S(1)} %fusion.64, f32[256,16]{0,1:T(8,128)S(1)} %get-tuple-element.375, bf16[256,8192]{1,0:T(8,128)(2,1)} %get-tuple-element.373, s32[]{:T(128)S(6)} %select_n.19), kind=kOutput, calls=%fused_computation.5.clone.1 | convolution fusion | flops 51641344 | bytes 1134596 | tf_op jit(solution)/shard_map/while/body/eval_jaxpr/dot_general | solution.py:41
  75.2 1.4 %fusion.62 = f32[1024,16]{0,1:T(8,128)S(1)} fusion(f32[256,16]{0,1:T(8,128)S(1)} %get-tuple-element.375, bf16[256,8192]{1,0:T(8,128)(2,1)} %get-tuple-element.373, s32[]{:T(128)S(6)} %select_n.19), kind=kOutput, calls=%fused_computation.7.clone.1 | convolution fusion | flops 50331648 | bytes 606212 | tf_op jit(solution)/shard_map/while/body/eval_jaxpr/dot_general | solution.py:37
  76.6 1.2 %custom-call.29 = f32[1,16,16]{1,2,0:T(8,128)S(1)} custom-call(f32[1,16,16]{2,1,0:T(8,128)S(1)} %bitcast_select_fusion.2), custom_call_target="InvertDiagBlocksLowerTriangular" | custom-call | tf_op jit(solution)/shard_map/while/body/eval_jaxpr/jit(_cho_solve)/triangular_solve | solution.py:40
  78.3 2.1 %multiply_reduce_fusion.3 = (f32[1024]{0:T(1024)S(1)}, bf16[256,1024]{1,0:T(8,128)(2,1)S(1)}) fusion(f32[16,1024]{1,0:T(8,128)S(1)} %fusion.64, f32[256,16]{0,1:T(8,128)S(1)} %get-tuple-element.375, bf16[256,8192]{1,0:T(8,128)(2,1)} %get-tuple-element.373, s32[]{:T(128)S(6)} %select_n.19), kind=kOutput, calls=%fused_computation.5.clone.1 | convolution fusion | flops 51641344 | bytes 1134596 | tf_op jit(solution)/shard_map/while/body/eval_jaxpr/dot_general | solution.py:41
  81.1 1.4 %fusion.62 = f32[1024,16]{0,1:T(8,128)S(1)} fusion(f32[256,16]{0,1:T(8,128)S(1)} %get-tuple-element.375, bf16[256,8192]{1,0:T(8,128)(2,1)} %get-tuple-element.373, s32[]{:T(128)S(6)} %select_n.19), kind=kOutput, calls=%fused_computation.7.clone.1 | convolution fusion | flops 50331648 | bytes 606212 | tf_op jit(solution)/shard_map/while/body/eval_jaxpr/dot_general | solution.py:37
  82.4 1.2 %custom-call.29 = f32[1,16,16]{1,2,0:T(8,128)S(1)} custom-call(f32[1,16,16]{2,1,0:T(8,128)S(1)} %bitcast_select_fusion.2), custom_call_target="InvertDiagBlocksLowerTriangular" | custom-call | tf_op jit(solution)/shard_map/while/body/eval_jaxpr/jit(_cho_solve)/triangular_solve | solution.py:40
  84.1 2.1 %multiply_reduce_fusion.3 = (f32[1024]{0:T(1024)S(1)}, bf16[256,1024]{1,0:T(8,128)(2,1)S(1)}) fusion(f32[16,1024]{1,0:T(8,128)S(1)} %fusion.64, f32[256,16]{0,1:T(8,128)S(1)} %get-tuple-element.375, bf16[256,8192]{1,0:T(8,128)(2,1)} %get-tuple-element.373, s32[]{:T(128)S(6)} %select_n.19), kind=kOutput, calls=%fused_computation.5.clone.1 | convolution fusion | flops 51641344 | bytes 1134596 | tf_op jit(solution)/shard_map/while/body/eval_jaxpr/dot_general | solution.py:41
  86.9 1.4 %fusion.62 = f32[1024,16]{0,1:T(8,128)S(1)} fusion(f32[256,16]{0,1:T(8,128)S(1)} %get-tuple-element.375, bf16[256,8192]{1,0:T(8,128)(2,1)} %get-tuple-element.373, s32[]{:T(128)S(6)} %select_n.19), kind=kOutput, calls=%fused_computation.7.clone.1 | convolution fusion | flops 50331648 | bytes 606212 | tf_op jit(solution)/shard_map/while/body/eval_jaxpr/dot_general | solution.py:37
  88.2 1.2 %custom-call.29 = f32[1,16,16]{1,2,0:T(8,128)S(1)} custom-call(f32[1,16,16]{2,1,0:T(8,128)S(1)} %bitcast_select_fusion.2), custom_call_target="InvertDiagBlocksLowerTriangular" | custom-call | tf_op jit(solution)/shard_map/while/body/eval_jaxpr/jit(_cho_solve)/triangular_solve | solution.py:40
  90.0 2.1 %multiply_reduce_fusion.3 = (f32[1024]{0:T(1024)S(1)}, bf16[256,1024]{1,0:T(8,128)(2,1)S(1)}) fusion(f32[16,1024]{1,0:T(8,128)S(1)} %fusion.64, f32[256,16]{0,1:T(8,128)S(1)} %get-tuple-element.375, bf16[256,8192]{1,0:T(8,128)(2,1)} %get-tuple-element.373, s32[]{:T(128)S(6)} %select_n.19), kind=kOutput, calls=%fused_computation.5.clone.1 | convolution fusion | flops 51641344 | bytes 1134596 | tf_op jit(solution)/shard_map/while/body/eval_jaxpr/dot_general | solution.py:41
  92.7 1.4 %fusion.62 = f32[1024,16]{0,1:T(8,128)S(1)} fusion(f32[256,16]{0,1:T(8,128)S(1)} %get-tuple-element.375, bf16[256,8192]{1,0:T(8,128)(2,1)} %get-tuple-element.373, s32[]{:T(128)S(6)} %select_n.19), kind=kOutput, calls=%fused_computation.7.clone.1 | convolution fusion | flops 50331648 | bytes 606212 | tf_op jit(solution)/shard_map/while/body/eval_jaxpr/dot_general | solution.py:37
  94.1 1.2 %custom-call.29 = f32[1,16,16]{1,2,0:T(8,128)S(1)} custom-call(f32[1,16,16]{2,1,0:T(8,128)S(1)} %bitcast_select_fusion.2), custom_call_target="InvertDiagBlocksLowerTriangular" | custom-call | tf_op jit(solution)/shard_map/while/body/eval_jaxpr/jit(_cho_solve)/triangular_solve | solution.py:40
  95.8 2.1 %multiply_reduce_fusion.3 = (f32[1024]{0:T(1024)S(1)}, bf16[256,1024]{1,0:T(8,128)(2,1)S(1)}) fusion(f32[16,1024]{1,0:T(8,128)S(1)} %fusion.64, f32[256,16]{0,1:T(8,128)S(1)} %get-tuple-element.375, bf16[256,8192]{1,0:T(8,128)(2,1)} %get-tuple-element.373, s32[]{:T(128)S(6)} %select_n.19), kind=kOutput, calls=%fused_computation.5.clone.1 | convolution fusion | flops 51641344 | bytes 1134596 | tf_op jit(solution)/shard_map/while/body/eval_jaxpr/dot_general | solution.py:41
  98.5 1.4 %fusion.62 = f32[1024,16]{0,1:T(8,128)S(1)} fusion(f32[256,16]{0,1:T(8,128)S(1)} %get-tuple-element.375, bf16[256,8192]{1,0:T(8,128)(2,1)} %get-tuple-element.373, s32[]{:T(128)S(6)} %select_n.19), kind=kOutput, calls=%fused_computation.7.clone.1 | convolution fusion | flops 50331648 | bytes 606212 | tf_op jit(solution)/shard_map/while/body/eval_jaxpr/dot_general | solution.py:37
  99.9 1.2 %custom-call.29 = f32[1,16,16]{1,2,0:T(8,128)S(1)} custom-call(f32[1,16,16]{2,1,0:T(8,128)S(1)} %bitcast_select_fusion.2), custom_call_target="InvertDiagBlocksLowerTriangular" | custom-call | tf_op jit(solution)/shard_map/while/body/eval_jaxpr/jit(_cho_solve)/triangular_solve | solution.py:40
  101.6 2.1 %multiply_reduce_fusion.3 = (f32[1024]{0:T(1024)S(1)}, bf16[256,1024]{1,0:T(8,128)(2,1)S(1)}) fusion(f32[16,1024]{1,0:T(8,128)S(1)} %fusion.64, f32[256,16]{0,1:T(8,128)S(1)} %get-tuple-element.375, bf16[256,8192]{1,0:T(8,128)(2,1)} %get-tuple-element.373, s32[]{:T(128)S(6)} %select_n.19), kind=kOutput, calls=%fused_computation.5.clone.1 | convolution fusion | flops 51641344 | bytes 1134596 | tf_op jit(solution)/shard_map/while/body/eval_jaxpr/dot_general | solution.py:41
  104.3 1.4 %fusion.62 = f32[1024,16]{0,1:T(8,128)S(1)} fusion(f32[256,16]{0,1:T(8,128)S(1)} %get-tuple-element.375, bf16[256,8192]{1,0:T(8,128)(2,1)} %get-tuple-element.373, s32[]{:T(128)S(6)} %select_n.19), kind=kOutput, calls=%fused_computation.7.clone.1 | convolution fusion | flops 50331648 | bytes 606212 | tf_op jit(solution)/shard_map/while/body/eval_jaxpr/dot_general | solution.py:37
  105.7 1.2 %custom-call.29 = f32[1,16,16]{1,2,0:T(8,128)S(1)} custom-call(f32[1,16,16]{2,1,0:T(8,128)S(1)} %bitcast_select_fusion.2), custom_call_target="InvertDiagBlocksLowerTriangular" | custom-call | tf_op jit(solution)/shard_map/while/body/eval_jaxpr/jit(_cho_solve)/triangular_solve | solution.py:40
  107.4 2.1 %multiply_reduce_fusion.3 = (f32[1024]{0:T(1024)S(1)}, bf16[256,1024]{1,0:T(8,128)(2,1)S(1)}) fusion(f32[16,1024]{1,0:T(8,128)S(1)} %fusion.64, f32[256,16]{0,1:T(8,128)S(1)} %get-tuple-element.375, bf16[256,8192]{1,0:T(8,128)(2,1)} %get-tuple-element.373, s32[]{:T(128)S(6)} %select_n.19), kind=kOutput, calls=%fused_computation.5.clone.1 | convolution fusion | flops 51641344 | bytes 1134596 | tf_op jit(solution)/shard_map/while/body/eval_jaxpr/dot_general | solution.py:41
  (68 shorter events, 12.7 us)
Async XLA Ops:
  7.2 56.5 %all-gather.2.cloned.1.call-start = ((), (), s32[]{:S(2)}) async-start(), calls=%async_computation.1 | async-start | bytes 4456448 | tf_op jit(solution)/shard_map/all_gather | solution.py:17
  9.6 34.7 %all-to-all-start = ((f32[16,16,112]{2,0,1:T(8,128)}), f32[16,16,112]{2,0,1:T(8,128)S(1)}, u32[]{:S(2)}, u32[]{:S(2)}) async-start(f32[16,16,112]{2,0,1:T(8,128)} %copy.15), calls=%async_computation | async-start | bytes 262144 | tf_op jit(solution)/shard_map/all_to_all | solution.py:18
Sparse Core Ops, SparseCore 0:
  10.1 53.4 all-gather.1
where the time goes:
time: 118 us; the launch traced here: 117 us
  matrix products  37.4 us (32%)
  blocking collectives  22.7 us (19%)
  waiting for transfers between devices  18.7 us (16%)
  other arithmetic  14.6 us (12%)
  between operations  14.1 us (12%)
  starting transfers between devices  7.45 us (6%)
  local copies, waits for them, and re-layouts  2.05 us (2%)
    all_gather x1, blocking collectives, local(): covars_all = lax.all_gather(covars, 'tile', axis=0, tiled=True)  22.7 us
    all_gather x1, waiting for transfers between devices, local(): dose_all = lax.all_gather(dosage, 'tile', axis=0, tiled=True)  18 us
    dot_general x8, matrix products, one_block(): jnp.dot(covars_all, beta_dose, precision=highest, preferred_element_type=...  17 us
    dot_general x8, matrix products, one_block(): jnp.dot(covars_all.T, dose_block, precision=highest, preferred_element_ty...  10.9 us
    another operation x16, other arithmetic, one_block(): beta_dose = jax.scipy.linalg.cho_solve((factor, True), cov_dose)  9.88 us
    all_to_all x1, starting transfers between devices, local(): lax.all_to_all(phenotypes, 'tile', split_axis=1, concat_axis=0, tiled=True)  7.41 us
    dot_general x8, matrix products, one_block(): lax.dot_general(pheno_bf, dose_resid.astype(jnp.bfloat16), (((0,), (0,)),...  4.42 us
    another operation x16, matrix products, one_block(): beta_dose = jax.scipy.linalg.cho_solve((factor, True), cov_dose)  3.7 us
  transfers between devices with their start and end apart: 2, of which 1 were waited for; matrix products, arithmetic and copies ran while one was open for 6% of the time, Pallas kernels for 0%

commit v1 on v0

--- a/solution.py
+++ b/solution.py
@@ -2,6 +2,13 @@
 import jax.numpy as jnp
 from jax import lax
 from jax.sharding import PartitionSpec as P
+from jax.lax import all_gather
+
+run_slots = lambda xin, inner_x: jnp.split(
+    all_gather(jnp.concatenate([xin, inner_x], 1), axis_name="tile", axis=0, tiled=True),
+    [xin.shape[1]],
+    1,
+)
 
 
 def local(dosage, covars, phenotypes):
@@ -13,8 +20,7 @@
     genes_all = phenotypes.shape[1]
     gene_own = genes_all // devices
     scale_root = jnp.sqrt(jnp.float32(samples))
-    covars_all = lax.all_gather(covars, "tile", axis=0, tiled=True)
-    dose_all = lax.all_gather(dosage, "tile", axis=0, tiled=True)
+    covars_all, dose_all = run_slots(covars, dosage)
     pheno_own = lax.all_to_all(phenotypes, "tile", split_axis=1, concat_axis=0, tiled=True)
     gram = jnp.dot(covars_all.T, covars_all, precision=highest, preferred_element_type=jnp.float32)
     factor = jnp.linalg.cholesky(gram)

time: 118 us -> 168 us (1.42)
  waiting for transfers between devices: 18.7 us -> 69.8 us
  blocking collectives: 22.7 us -> 0 us
  local copies, waits for them, and re-layouts: 2.05 us -> 11.8 us
  matrix products: 37.4 us -> 45.6 us
  other arithmetic: 14.6 us -> 17.3 us
    all_gather x1, waiting for transfers between devices: 18 us -> 61.7 us  [all_gather(jnp.concatenate([xin, inner_x], 1), axis_name='tile', axis=0,...]
    all_gather x1 -> x0, blocking collectives: 22.7 us -> none  [local(): covars_all = lax.all_gather(covars, 'tile', axis=0, tiled=True)]
    split x0 -> x2, local copies, waits for them, and re-layouts: none -> 9.79 us  [jnp.split(all_gather(jnp.concatenate([xin, inner_x], 1), axis_name='tile'...]
    all_to_all x1, waiting for transfers between devices: 0.01 us -> 8.06 us  [local(): lax.all_to_all(phenotypes, 'tile', split_axis=1, concat_axis=0, tiled=True)]
    dot_general x8, matrix products: 10.9 us -> 15 us  [one_block(): jnp.dot(covars_all.T, dose_block, precision=highest, preferred_element_ty...]
    concatenate x0 -> x1, other arithmetic: none -> 1.74 us  [jnp.concatenate([xin, inner_x], 1)]
  transfers between devices with their start and end apart: 2 -> 2, of which waited for: 1 -> 2; matrix products, arithmetic and copies ran while one was open for 6% -> 0% of each run, Pallas kernels for 0% -> 0%
where the time goes in v1:
time: 168 us; the launch traced here: 167 us
  waiting for transfers between devices  69.8 us (42%)
  matrix products  45.6 us (27%)
  other arithmetic  17.3 us (10%)
  between operations  14.1 us (8%)
  local copies, waits for them, and re-layouts  11.8 us (7%)
  starting transfers between devices  7.45 us (4%)
    all_gather x1, waiting for transfers between devices, all_gather(jnp.concatenate([xin, inner_x], 1), axis_name='tile', axis=0,...  61.7 us
    dot_general x8, matrix products, one_block(): jnp.dot(covars_all, beta_dose, precision=highest, preferred_element_type=...  18.3 us
    dot_general x8, matrix products, one_block(): jnp.dot(covars_all.T, dose_block, precision=highest, preferred_element_ty...  15 us
    another operation x16, other arithmetic, one_block(): beta_dose = jax.scipy.linalg.cho_solve((factor, True), cov_dose)  9.88 us
    split x2, local copies, waits for them, and re-layouts, jnp.split(all_gather(jnp.concatenate([xin, inner_x], 1), axis_name='tile'...  9.79 us
    all_to_all x1, waiting for transfers between devices, local(): lax.all_to_all(phenotypes, 'tile', split_axis=1, concat_axis=0, tiled=True)  8.06 us
    all_to_all x1, starting transfers between devices, local(): lax.all_to_all(phenotypes, 'tile', split_axis=1, concat_axis=0, tiled=True)  7.41 us
    dot_general x8, matrix products, one_block(): lax.dot_general(pheno_bf, dose_resid.astype(jnp.bfloat16), (((0,), (0,)),...  4.43 us
  transfers between devices with their start and end apart: 2, of which 2 were waited for; matrix products, arithmetic and copies ran while one was open for 0% of the time, Pallas kernels for 0%

profile of v1, /device:TPU:0, one launch (start us, length us, event | category | flops | bytes accessed | tf_op | source)
XLA Modules:
  0.0 166.7 jit_solution(1436347254316864222)
XLA Ops:
  8.2 1.7 %pad_maximum_fusion = f32[16,8208]{1,0:T(8,128)} fusion(f32[16,8192]{1,0:T(8,128)S(1)} %convert_element_type.16, f32[16,16]{1,0:T(8,128)} %param.6), kind=kLoop, calls=%fused_computation.24 | loop fusion | flops 131328 | bytes 1050624 | tf_op jit(solution)/shard_map/concatenate | solution.py:8
  11.7 7.4 %all-to-all-start = ((f32[16,16,112]{2,0,1:T(8,128)}), f32[16,16,112]{2,0,1:T(8,128)S(1)}, u32[]{:S(2)}, u32[]{:S(2)}) async-start(f32[16,16,112]{2,0,1:T(8,128)} %copy.19), calls=%async_computation | async-start | bytes 262144 | tf_op jit(solution)/shard_map/all_to_all | solution.py:24
  19.1 8.1 %all-to-all-done = f32[16,16,112]{2,0,1:T(8,128)S(1)} async-done(((f32[16,16,112]{2,0,1:T(8,128)}), f32[16,16,112]{2,0,1:T(8,128)S(1)}, u32[]{:S(2)}, u32[]{:S(2)}) %all-to-all-start) | async-done | bytes 114720 | tf_op jit(solution)/shard_map/all_to_all | solution.py:24
  27.3 61.7 %all-gather.2.cloned.1.call-done = f32[256,8208]{1,0:T(8,128)} async-done(((f32[16,8208]{1,0:T(8,128)}), f32[256,8208]{1,0:T(8,128)}) %all-gather.2.cloned.1.call-update) | async-done | bytes 8405008 | tf_op jit(solution)/shard_map/all_gather | solution.py:8
  89.0 1.3 fusion.22
  90.4 1.5 cholesky.18
  93.2 1.2 custom-call.24
  94.5 1.3 fusion.20
  96.1 1.3 multiply_reduce_fusion.1
  98.5 8.9 %split.8 = f32[256,8192]{1,0:T(8,128)} slice(f32[256,8208]{1,0:T(8,128)} %all-gather.2.cloned.1.call-done), slice={[0:256], [16:8208]} | slice | bytes 16777216 | tf_op jit(solution)/shard_map/split | solution.py:7
  107.4 51.9 %while.18 = (s32[]{:T(128)}, f32[112]{0:T(128)S(1)}, f32[112]{0:T(128)S(1)}, f32[256,8192]{1,0:T(8,128)}, f32[16,16]{1,0:T(8,128)S(1)}, /*index=5*/f32[256,16]{0...) while((s32[]{:T(128)}, f32[112]{0:T(128)S(1)}, ...), condition=%wide.region_7.8_spmd.clone, body=%wide.region_3.7_spmd.clone.sunk | while | flops 167986912 | bytes 3653749 | solution.py:65
  107.4 1.9 %fusion.60 = f32[1024,16]{0,1:T(8,128)S(1)} fusion(f32[256,16]{0,1:T(8,128)S(1)} %get-tuple-element.375, f32[256,8192]{1,0:T(8,128)} %get-tuple-element.373, s32[]{:T(128)S(6)} %select_n.19), kind=kOutput, calls=%fused_computation.6.clone.1 | convolution fusion | flops 50331648 | bytes 1130500 | tf_op jit(solution)/shard_map/while/body/eval_jaxpr/dot_general | solution.py:43
  109.3 1.2 custom-call.29
  111.0 2.3 %multiply_reduce_fusion.3 = (f32[1024]{0:T(1024)S(1)}, bf16[256,1024]{1,0:T(8,128)(2,1)S(1)}) fusion(f32[16,1024]{1,0:T(8,128)S(1)} %fusion.62, f32[256,16]{0,1:T(8,128)S(1)} %get-tuple-element.375, f32[256,8192]{1,0:T(8,128)} %get-tuple-element.373, s32[]{:T(128)S(6)} %select_n.19), kind=kOutput, calls=%fused_computation.5.clone.1 | convolution fusion | flops 51379200 | bytes 1658884 | tf_op jit(solution)/shard_map/while/body/eval_jaxpr/dot_general | solution.py:47
  113.9 1.9 %fusion.60 = f32[1024,16]{0,1:T(8,128)S(1)} fusion(f32[256,16]{0,1:T(8,128)S(1)} %get-tuple-element.375, f32[256,8192]{1,0:T(8,128)} %get-tuple-element.373, s32[]{:T(128)S(6)} %select_n.19), kind=kOutput, calls=%fused_computation.6.clone.1 | convolution fusion | flops 50331648 | bytes 1130500 | tf_op jit(solution)/shard_map/while/body/eval_jaxpr/dot_general | solution.py:43
  115.8 1.2 custom-call.29
  117.5 2.3 %multiply_reduce_fusion.3 = (f32[1024]{0:T(1024)S(1)}, bf16[256,1024]{1,0:T(8,128)(2,1)S(1)}) fusion(f32[16,1024]{1,0:T(8,128)S(1)} %fusion.62, f32[256,16]{0,1:T(8,128)S(1)} %get-tuple-element.375, f32[256,8192]{1,0:T(8,128)} %get-tuple-element.373, s32[]{:T(128)S(6)} %select_n.19), kind=kOutput, calls=%fused_computation.5.clone.1 | convolution fusion | flops 51379200 | bytes 1658884 | tf_op jit(solution)/shard_map/while/body/eval_jaxpr/dot_general | solution.py:47
  120.4 1.9 %fusion.60 = f32[1024,16]{0,1:T(8,128)S(1)} fusion(f32[256,16]{0,1:T(8,128)S(1)} %get-tuple-element.375, f32[256,8192]{1,0:T(8,128)} %get-tuple-element.373, s32[]{:T(128)S(6)} %select_n.19), kind=kOutput, calls=%fused_computation.6.clone.1 | convolution fusion | flops 50331648 | bytes 1130500 | tf_op jit(solution)/shard_map/while/body/eval_jaxpr/dot_general | solution.py:43
  122.3 1.2 custom-call.29
  124.0 2.3 %multiply_reduce_fusion.3 = (f32[1024]{0:T(1024)S(1)}, bf16[256,1024]{1,0:T(8,128)(2,1)S(1)}) fusion(f32[16,1024]{1,0:T(8,128)S(1)} %fusion.62, f32[256,16]{0,1:T(8,128)S(1)} %get-tuple-element.375, f32[256,8192]{1,0:T(8,128)} %get-tuple-element.373, s32[]{:T(128)S(6)} %select_n.19), kind=kOutput, calls=%fused_computation.5.clone.1 | convolution fusion | flops 51379200 | bytes 1658884 | tf_op jit(solution)/shard_map/while/body/eval_jaxpr/dot_general | solution.py:47
  126.8 1.9 %fusion.60 = f32[1024,16]{0,1:T(8,128)S(1)} fusion(f32[256,16]{0,1:T(8,128)S(1)} %get-tuple-element.375, f32[256,8192]{1,0:T(8,128)} %get-tuple-element.373, s32[]{:T(128)S(6)} %select_n.19), kind=kOutput, calls=%fused_computation.6.clone.1 | convolution fusion | flops 50331648 | bytes 1130500 | tf_op jit(solution)/shard_map/while/body/eval_jaxpr/dot_general | solution.py:43
  128.7 1.2 custom-call.29
  130.4 2.3 %multiply_reduce_fusion.3 = (f32[1024]{0:T(1024)S(1)}, bf16[256,1024]{1,0:T(8,128)(2,1)S(1)}) fusion(f32[16,1024]{1,0:T(8,128)S(1)} %fusion.62, f32[256,16]{0,1:T(8,128)S(1)} %get-tuple-element.375, f32[256,8192]{1,0:T(8,128)} %get-tuple-element.373, s32[]{:T(128)S(6)} %select_n.19), kind=kOutput, calls=%fused_computation.5.clone.1 | convolution fusion | flops 51379200 | bytes 1658884 | tf_op jit(solution)/shard_map/while/body/eval_jaxpr/dot_general | solution.py:47
  133.3 1.9 %fusion.60 = f32[1024,16]{0,1:T(8,128)S(1)} fusion(f32[256,16]{0,1:T(8,128)S(1)} %get-tuple-element.375, f32[256,8192]{1,0:T(8,128)} %get-tuple-element.373, s32[]{:T(128)S(6)} %select_n.19), kind=kOutput, calls=%fused_computation.6.clone.1 | convolution fusion | flops 50331648 | bytes 1130500 | tf_op jit(solution)/shard_map/while/body/eval_jaxpr/dot_general | solution.py:43
  135.2 1.2 custom-call.29
  136.9 2.3 %multiply_reduce_fusion.3 = (f32[1024]{0:T(1024)S(1)}, bf16[256,1024]{1,0:T(8,128)(2,1)S(1)}) fusion(f32[16,1024]{1,0:T(8,128)S(1)} %fusion.62, f32[256,16]{0,1:T(8,128)S(1)} %get-tuple-element.375, f32[256,8192]{1,0:T(8,128)} %get-tuple-element.373, s32[]{:T(128)S(6)} %select_n.19), kind=kOutput, calls=%fused_computation.5.clone.1 | convolution fusion | flops 51379200 | bytes 1658884 | tf_op jit(solution)/shard_map/while/body/eval_jaxpr/dot_general | solution.py:47
  139.8 1.9 %fusion.60 = f32[1024,16]{0,1:T(8,128)S(1)} fusion(f32[256,16]{0,1:T(8,128)S(1)} %get-tuple-element.375, f32[256,8192]{1,0:T(8,128)} %get-tuple-element.373, s32[]{:T(128)S(6)} %select_n.19), kind=kOutput, calls=%fused_computation.6.clone.1 | convolution fusion | flops 50331648 | bytes 1130500 | tf_op jit(solution)/shard_map/while/body/eval_jaxpr/dot_general | solution.py:43
  143.4 2.3 %multiply_reduce_fusion.3 = (f32[1024]{0:T(1024)S(1)}, bf16[256,1024]{1,0:T(8,128)(2,1)S(1)}) fusion(f32[16,1024]{1,0:T(8,128)S(1)} %fusion.62, f32[256,16]{0,1:T(8,128)S(1)} %get-tuple-element.375, f32[256,8192]{1,0:T(8,128)} %get-tuple-element.373, s32[]{:T(128)S(6)} %select_n.19), kind=kOutput, calls=%fused_computation.5.clone.1 | convolution fusion | flops 51379200 | bytes 1658884 | tf_op jit(solution)/shard_map/while/body/eval_jaxpr/dot_general | solution.py:47
  146.3 1.9 %fusion.60 = f32[1024,16]{0,1:T(8,128)S(1)} fusion(f32[256,16]{0,1:T(8,128)S(1)} %get-tuple-element.375, f32[256,8192]{1,0:T(8,128)} %get-tuple-element.373, s32[]{:T(128)S(6)} %select_n.19), kind=kOutput, calls=%fused_computation.6.clone.1 | convolution fusion | flops 50331648 | bytes 1130500 | tf_op jit(solution)/shard_map/while/body/eval_jaxpr/dot_general | solution.py:43
  149.9 2.3 %multiply_reduce_fusion.3 = (f32[1024]{0:T(1024)S(1)}, bf16[256,1024]{1,0:T(8,128)(2,1)S(1)}) fusion(f32[16,1024]{1,0:T(8,128)S(1)} %fusion.62, f32[256,16]{0,1:T(8,128)S(1)} %get-tuple-element.375, f32[256,8192]{1,0:T(8,128)} %get-tuple-element.373, s32[]{:T(128)S(6)} %select_n.19), kind=kOutput, calls=%fused_computation.5.clone.1 | convolution fusion | flops 51379200 | bytes 1658884 | tf_op jit(solution)/shard_map/while/body/eval_jaxpr/dot_general | solution.py:47
  152.8 1.9 %fusion.60 = f32[1024,16]{0,1:T(8,128)S(1)} fusion(f32[256,16]{0,1:T(8,128)S(1)} %get-tuple-element.375, f32[256,8192]{1,0:T(8,128)} %get-tuple-element.373, s32[]{:T(128)S(6)} %select_n.19), kind=kOutput, calls=%fused_computation.6.clone.1 | convolution fusion | flops 50331648 | bytes 1130500 | tf_op jit(solution)/shard_map/while/body/eval_jaxpr/dot_general | solution.py:43
  156.4 2.3 %multiply_reduce_fusion.3 = (f32[1024]{0:T(1024)S(1)}, bf16[256,1024]{1,0:T(8,128)(2,1)S(1)}) fusion(f32[16,1024]{1,0:T(8,128)S(1)} %fusion.62, f32[256,16]{0,1:T(8,128)S(1)} %get-tuple-element.375, f32[256,8192]{1,0:T(8,128)} %get-tuple-element.373, s32[]{:T(128)S(6)} %select_n.19), kind=kOutput, calls=%fused_computation.5.clone.1 | convolution fusion | flops 51379200 | bytes 1658884 | tf_op jit(solution)/shard_map/while/body/eval_jaxpr/dot_general | solution.py:47
  (71 shorter events, 18.2 us)
Async XLA Ops:
  7.2 81.9 %all-gather.2.cloned.1.call-start = ((), (), s32[]{:S(2)}) async-start(), calls=%async_computation.1 | async-start | bytes 9052160 | tf_op jit(solution)/shard_map/all_gather | solution.py:8
  11.7 15.5 %all-to-all-start = ((f32[16,16,112]{2,0,1:T(8,128)}), f32[16,16,112]{2,0,1:T(8,128)S(1)}, u32[]{:S(2)}, u32[]{:S(2)}) async-start(f32[16,16,112]{2,0,1:T(8,128)} %copy.19), calls=%async_computation | async-start | bytes 262144 | tf_op jit(solution)/shard_map/all_to_all | solution.py:24
Sparse Core Ops, SparseCore 0:
  10.3 78.7 all-gather.1
